TPU v7x, 32 devices: a whole 2x2x4 slice. The times are simulated.
32 devices in a mesh: outer: 2 (over core), dp: 4 (over z), tensor: 4 (over y, x).
Axes of the slice: x: 2, y: 2, z: 4, core: 2. Of those that a mesh axis runs over, the one named last changes fastest.
Arguments:
- attn: bfloat16 [2048, 8192], P(('outer', 'dp'), 'tensor'), may hold values from -6 to 6
- out_weight: bfloat16 [8192, 8192], P(None, 'tensor'), may hold values from -0.0625 to 0.0625
- resid: bfloat16 [2048, 8192], P(('outer', 'dp'), 'tensor'), may hold values from -8 to 8
- norm_gain: bfloat16 [8192], P('tensor'), may hold values from 0.5 to 1.5
- head: bfloat16 [8192], P('tensor'), may hold values from -1 to 1
- lengths: int32 [32], P(('outer', 'dp')), may hold values from 1 to 64
- pairs: int32 [32, 2], P(('outer', 'dp')), may hold values from 0 to 3, as said below
- pair_valid: int32 [32], P(('outer', 'dp')), may hold values from 0 to 1, as said below
- loss_scale: float32 [1], replicated, may hold values from 1024 to 8192
Outputs:
- loss: float32 [1], replicated
- grad_out_proj: float32 [8192, 8192], P(('outer', 'dp'), 'tensor')
- grad_gain: float32 [8192], P('tensor')
- grad_head: float32 [8192], P('tensor')
Inputs may be any that keep to these rules, and one draw needn't show every extreme that they name: `pairs`: in each pair the two numbers differ; the first pair of each replica is valid. `pair_valid`: the first of each replica's 4 entries is 1.
All inputs are finite; a program needn't handle non-finite values.
Results may differ from a plain program's by a relative error of at most 0.003.
Values may be sent and summed in bfloat16 or wider, within the bound.
A program may use at most 128 MiB of HBM per device.

v0:
```python
import jax
import jax.numpy as jnp
from jax import lax
from jax.sharding import PartitionSpec as P


def shards(attn, out_weight, resid, norm_gain, head, lengths, pairs, pair_valid, loss_scale):
    f32 = jnp.float32
    tok_dev = attn.shape[0]
    feats = resid.shape[1]
    tensor = lax.axis_size("tensor")
    width = feats * tensor
    seqs_dev = lengths.shape[0]
    seq_len = tok_dev // seqs_dev
    valid = pair_valid.astype(f32)
    count = lax.psum(jnp.sum(valid), ("outer", "dp"))
    part = lax.dot_general(out_weight, attn, (((1,), (1,)), ((), ())), preferred_element_type=f32)
    part = part.astype(jnp.bfloat16).reshape(tensor, feats, tok_dev)
    part = lax.all_to_all(part, "tensor", split_axis=0, concat_axis=0, tiled=True)
    z = resid.astype(f32).T + jnp.sum(part.astype(f32), axis=0)
    gain = norm_gain.astype(f32)[:, None]
    headv = head.astype(f32)[:, None]
    both = headv * gain
    sums = lax.psum(jnp.stack([jnp.sum(z * z, axis=0), jnp.sum(z * both, axis=0)]), "tensor")
    inv = 1.0 / jnp.sqrt(sums[0] / width + 1e-05)
    score = sums[1] * inv
    position = jnp.arange(tok_dev)
    seq_of = position // seq_len
    within = position % seq_len
    member = (within[:, None] < lengths[None, :]) & (
        seq_of[:, None] == jnp.arange(seqs_dev)[None, :]
    )
    pooling = member.astype(f32) / lengths.astype(f32)[None, :]
    reward = jnp.sum(pooling * score[:, None], axis=0)
    choose = jnp.arange(seqs_dev)[None, :]
    select = (pairs[:, 0:1] == choose).astype(f32) - (pairs[:, 1:2] == choose).astype(f32)
    margin = jnp.sum(select * reward[None, :], axis=1)
    loss_part = jnp.sum(valid * jax.nn.softplus(-margin))
    dmargin = -loss_scale[0] * valid * jax.nn.sigmoid(-margin) / count
    dreward = jnp.sum(dmargin[:, None] * select, axis=0)
    dscore = jnp.sum(pooling * dreward[None, :], axis=1)
    weight = inv * dscore
    dproj = weight[None, :] * both - z * (inv**3 * dscore * sums[1] / width)[None, :]
    dproj = dproj.astype(jnp.bfloat16)
    zsum = jnp.sum(z * weight[None, :], axis=1)
    gathered = lax.all_gather(dproj, "tensor", axis=0, tiled=True)
    exchanged = lax.all_to_all(gathered, ("outer", "dp"), split_axis=0, concat_axis=1, tiled=True)
    grad_out_proj = jnp.dot(
        exchanged,
        lax.all_gather(attn, ("outer", "dp"), axis=0, tiled=True),
        preferred_element_type=f32,
    )
    zsum, loss_sum = lax.psum((zsum, loss_part), ("outer", "dp"))
    loss = (loss_sum / count).reshape(1)
    return (loss, grad_out_proj, zsum * headv[:, 0], zsum * gain[:, 0])


def solution(mesh):
    return jax.shard_map(
        shards,
        mesh=mesh,
        in_specs=(
            P(("outer", "dp"), "tensor"),
            P(None, "tensor"),
            P(("outer", "dp"), "tensor"),
            P("tensor"),
            P("tensor"),
            P(("outer", "dp")),
            P(("outer", "dp"), None),
            P(("outer", "dp")),
            P(),
        ),
        out_specs=(P(), P(("outer", "dp"), "tensor"), P("tensor"), P("tensor")),
        check_vma=False,
    )
```

profile of v0, /device:TPU:0, one launch (start us, length us, event | category | flops | bytes accessed | tf_op | source)
XLA Modules:
  0.0 368.8 jit_solution(16129040595212171715)
XLA Ops:
  7.2 16.7 %convolution_convert_fusion = bf16[8192,256]{1,0:T(8,128)(2,1)} fusion(bf16[8192,2048]{1,0:T(8,128)(2,1)} %param.10, bf16[256,2048]{1,0:T(8,128)(2,1)} %param.9), kind=kOutput, calls=%fused_computation | convolution fusion | flops 8592031744 | bytes 38797312 | tf_op jit(solution)/shard_map/dot_general | solution.py:17
  23.9 0.0 copy-start
  23.9 0.0 copy-start.3
  23.9 0.0 copy-start.5
  23.9 0.0 copy-start.1
  23.9 0.0 copy-start.2
  23.9 5.3 %all-to-all-start = ((bf16[4,2048,256]{2,1,0:T(8,128)(2,1)}), bf16[4,2048,256]{2,1,0:T(8,128)(2,1)}, u32[]{:S(2)}, u32[]{:S(2)}) async-start(bf16[4,2048,256]{2,1,0:T(8,128)(2,1)} %bitcast.31), calls=%async_computation | async-start | bytes 8388608 | tf_op jit(solution)/shard_map/all_to_all | solution.py:19
  29.3 0.0 all-gather.3.cloned.1.call-start
  29.3 0.0 copy-done
  29.3 0.5 copy.15
  29.8 0.0 copy-done.3
  30.5 0.0 copy-done.5
  30.5 0.0 copy-done.1
  30.5 0.0 copy-done.2
  30.6 0.0 copy-start.4
  30.6 47.4 %all-to-all-done = bf16[4,2048,256]{2,1,0:T(8,128)(2,1)} async-done(((bf16[4,2048,256]{2,1,0:T(8,128)(2,1)}), bf16[4,2048,256]{2,1,0:T(8,128)(2,1)}, u32[]{:S(2)}, u32[]{:S(2)}) %all-to-all-start) | async-done | bytes 4194336 | tf_op jit(solution)/shard_map/all_to_all | solution.py:19
  77.9 3.0 convert_reduce_fusion
  80.9 0.5 multiply_reduce_fusion.2
  81.4 8.9 %psum.28 = f32[2,256]{1,0:T(2,128)S(1)} all-reduce(f32[2,256]{1,0:T(2,128)S(1)} %pad_maximum_fusion), channel_id=1, replica_groups=mesh['outer'=2,'dp'=4,'tensor'=4] {'tensor'}, use_global_device_ids=true, to_apply=%region_3.0 | all-reduce | flops 512 | bytes 4096 | tf_op jit(solution)/shard_map/psum | solution.py:24
  90.3 0.2 multiply_reduce_fusion.4
  90.5 0.2 multiply_reduce_fusion.6
  90.7 0.0 copy-done.4
  90.7 0.6 convert_reduce_fusion.1
  91.3 16.2 %psum.30 = f32[]{:T(128)} all-reduce(f32[]{:T(128)} %get-tuple-element.6), channel_id=1, replica_groups=mesh['outer'=2,'dp'=4,'tensor'=4] {'outer','dp'}, use_global_device_ids=true, to_apply=%region_9.10 | all-reduce | flops 1 | bytes 8 | tf_op jit(solution)/shard_map/psum | solution.py:16
  107.5 0.7 fusion.9
  108.2 0.1 multiply_reduce_fusion.5
  108.3 0.1 multiply_reduce_fusion.3
  108.4 1.5 subtract_convert_fusion
  109.9 0.0 all-gather.3.cloned.1.call-update
  109.9 0.0 all-gather.5.cloned.1.call-start
  110.0 0.7 all-gather.5.cloned.1.call-update
  110.7 50.8 %all-gather.3.cloned.1.call-done = bf16[8192,256]{1,0:T(8,128)(2,1)} async-done(((bf16[2048,256]{1,0:T(8,128)(2,1)}), bf16[8192,256]{1,0:T(8,128)(2,1)}) %all-gather.3.cloned.1.call-update) | async-done | bytes 4194320 | tf_op jit(solution)/shard_map/all_gather | solution.py:46
  161.5 4.6 %all-to-all-start.1 = ((bf16[8,1024,256]{2,1,0:T(8,128)(2,1)}), bf16[8,1024,256]{2,1,0:T(8,128)(2,1)}, u32[]{:S(2)}, u32[]{:S(2)}) async-start(bf16[8,1024,256]{2,1,0:T(8,128)(2,1)} %bitcast.30), calls=%async_computation.1 | async-start | bytes 8388608 | tf_op jit(solution)/shard_map/all_to_all | solution.py:47
  166.1 171.7 %all-reduce = (f32[]{:T(128)}, f32[2048]{0:T(1024)S(1)}) all-reduce(f32[]{:T(128)} %get-tuple-element.7, f32[2048]{0:T(1024)S(1)} %get-tuple-element.11), channel_id=1, replica_groups=mesh['outer'=2,'dp'=4,'tensor'=4] {'outer','dp'}, use_global_device_ids=true, to_apply=%region_7.8 | all-reduce | flops 2049 | bytes 16392 | tf_op jit(solution)/shard_map/psum | solution.py:53
  339.1 0.6 convert_multiply_fusion
  339.7 0.0 all-to-all-done.1
  339.7 6.5 %copy.16 = bf16[1024,8,256]{0,2,1:T(8,128)(2,1)} copy(bf16[1024,8,256]{2,0,1:T(8,128)(2,1)} %bitcast.13) | data formatting | bytes 8388608 | tf_op jit(solution)/shard_map/all_to_all | solution.py:47
  346.2 0.0 all-gather.5.cloned.1.call-done
  346.2 14.6 %fusion.11 = f32[1024,2048]{1,0:T(8,128)} fusion(bf16[1024,2048]{0,1:T(8,128)(2,1)} %bitcast.32, bf16[2048,2048]{1,0:T(8,128)(2,1)} %all-gather.5.cloned.1.call-done), kind=kOutput, calls=%fused_computation.44 | convolution fusion | flops 8589934592 | bytes 20971520 | tf_op jit(solution)/shard_map/dot_general | solution.py:48
  (7 shorter events, 0.1 us)
Async XLA Ops:
  23.9 5.4 %copy-start = (bf16[256,2048]{1,0:T(8,128)(2,1)S(1)}, bf16[256,2048]{1,0:T(8,128)(2,1)}, u32[]{:S(2)}) copy-start(bf16[256,2048]{1,0:T(8,128)(2,1)} %param.11) | copy-start | bytes 3145732
  23.9 5.9 %copy-start.3 = (s32[4]{0:T(128)S(1)}, s32[4]{0:T(128)}, u32[]{:S(2)}) copy-start(s32[4]{0:T(128)} %param.14) | copy-start | bytes 52
  23.9 6.6 %copy-start.5 = (s32[4,2]{0,1:T(2,128)S(1)}, s32[4,2]{0,1:T(2,128)}, u32[]{:S(2)}) copy-start(s32[4,2]{0,1:T(2,128)} %param.15) | copy-start | bytes 100
  23.9 6.6 %copy-start.1 = (bf16[2048]{0:T(1024)(128)(2,1)S(1)}, bf16[2048]{0:T(1024)(128)(2,1)}, u32[]{:S(2)}) copy-start(bf16[2048]{0:T(1024)(128)(2,1)} %param.12) | copy-start | bytes 12292
  23.9 6.6 %copy-start.2 = (bf16[2048]{0:T(1024)(128)(2,1)S(1)}, bf16[2048]{0:T(1024)(128)(2,1)}, u32[]{:S(2)}) copy-start(bf16[2048]{0:T(1024)(128)(2,1)} %param.13) | copy-start | bytes 12292
  23.9 54.0 %all-to-all-start = ((bf16[4,2048,256]{2,1,0:T(8,128)(2,1)}), bf16[4,2048,256]{2,1,0:T(8,128)(2,1)}, u32[]{:S(2)}, u32[]{:S(2)}) async-start(bf16[4,2048,256]{2,1,0:T(8,128)(2,1)} %bitcast.31), calls=%async_computation | async-start | bytes 8388608 | tf_op jit(solution)/shard_map/all_to_all | solution.py:19
  29.3 132.2 %all-gather.3.cloned.1.call-start = ((), (), s32[]{:S(2)}) async-start(), calls=%async_computation.2 | async-start | bytes 5242880 | tf_op jit(solution)/shard_map/all_gather | solution.py:46
  30.6 60.2 %copy-start.4 = (s32[4]{0:T(128)S(1)}, s32[4]{0:T(128)}, u32[]{:S(2)}) copy-start(s32[4]{0:T(128)} %param.16) | copy-start | bytes 52
  109.9 236.3 %all-gather.5.cloned.1.call-start = ((), (), s32[]{:S(2)}) async-start(), calls=%async_computation.3 | async-start | bytes 9437184 | tf_op jit(solution)/shard_map/all_gather | solution.py:50
  161.5 178.2 %all-to-all-start.1 = ((bf16[8,1024,256]{2,1,0:T(8,128)(2,1)}), bf16[8,1024,256]{2,1,0:T(8,128)(2,1)}, u32[]{:S(2)}, u32[]{:S(2)}) async-start(bf16[8,1024,256]{2,1,0:T(8,128)(2,1)} %bitcast.30), calls=%async_computation.1 | async-start | bytes 8388608 | tf_op jit(solution)/shard_map/all_to_all | solution.py:47
Sparse Core Ops, SparseCore 0:
  110.0 51.4 all-gather.2
  163.1 160.7 all-gather.4
where the time goes:
time: 369 us
  blocking collectives  197 us (53%)
  waiting for transfers between devices  98.9 us (27%)
  matrix products  31.4 us (9%)
  between operations  17.3 us (5%)
  starting transfers between devices  9.99 us (3%)
  other arithmetic  7.44 us (2%)
  local copies, waits for them, and re-layouts  7.01 us (2%)
    psum x1, blocking collectives, shards(): zsum, loss_sum = lax.psum((zsum, loss_part), ('outer', 'dp'))  172 us
    all_gather x1, waiting for transfers between devices, shards(): gathered = lax.all_gather(dproj, 'tensor', axis=0, tiled=True)  50.8 us
    all_to_all x1, waiting for transfers between devices, shards(): lax.all_to_all(part, 'tensor', split_axis=0, concat_axis=0, tiled=True)  47.4 us
    dot_general x1, matrix products, shards(): lax.dot_general(out_weight, attn, (((1,), (1,)), ((), ())), preferred_ele...  16.7 us
    psum x1, blocking collectives, shards(): count = lax.psum(jnp.sum(valid), ('outer', 'dp'))  16.2 us
    dot_general x1, matrix products, shards(): jnp.dot(exchanged, lax.all_gather(attn, ('outer', 'dp'), axis=0, tiled=Tr...  14.6 us
    psum x1, blocking collectives, shards(): lax.psum(jnp.stack([jnp.sum(z * z, axis=0), jnp.sum(z * both, axis=0)]),...  8.91 us
  transfers between devices with their start and end apart: 4, of which 2 were waited for; matrix products, arithmetic and copies ran while one was open for 2% of the time, Pallas kernels for 0%

commit v1 on v0

--- a/solution.py
+++ b/solution.py
@@ -2,6 +2,23 @@
 import jax.numpy as jnp
 from jax import lax
 from jax.sharding import PartitionSpec as P
+
+
+def in_order(blocks, dim):
+    blocks = jnp.moveaxis(blocks, 0, dim)
+    lengths = blocks.shape
+    return blocks.reshape(*lengths[:dim], lengths[dim] * lengths[dim + 1], *lengths[dim + 2 :])
+
+
+def ring_gather(x, axis, dim):
+    size = lax.axis_size(axis)
+    forward = [(i, (i + 1) % size) for i in range(size)]
+    parts = [x]
+    while len(parts) < size:
+        parts.append(lax.ppermute(parts[-1], axis, forward))
+    index = lax.axis_index(axis)
+    parts = jnp.stack(parts)[(index - jnp.arange(size)) % size]
+    return in_order(parts, dim)
 
 
 def shards(attn, out_weight, resid, norm_gain, head, lengths, pairs, pair_valid, loss_scale):
@@ -43,7 +60,7 @@
     dproj = weight[None, :] * both - z * (inv**3 * dscore * sums[1] / width)[None, :]
     dproj = dproj.astype(jnp.bfloat16)
     zsum = jnp.sum(z * weight[None, :], axis=1)
-    gathered = lax.all_gather(dproj, "tensor", axis=0, tiled=True)
+    gathered = ring_gather(dproj, "tensor", 0)
     exchanged = lax.all_to_all(gathered, ("outer", "dp"), split_axis=0, concat_axis=1, tiled=True)
     grad_out_proj = jnp.dot(
         exchanged,

time: 369 us -> 341 us (0.924)
  blocking collectives: 197 us -> 134 us
  waiting for transfers between devices: 98.9 us -> 125 us
  local copies, waits for them, and re-layouts: 7.01 us -> 13 us
    ppermute x0 -> x3, waiting for transfers between devices: none -> 78 us  [ring_gather(): parts.append(lax.ppermute(parts[-1], axis, forward))]
    psum x1, blocking collectives: 172 us -> 104 us  [shards(): zsum, loss_sum = lax.psum((zsum, loss_part), ('outer', 'dp'))]
    all_gather x1 -> x0, waiting for transfers between devices: 50.8 us -> none  [shards(): gathered = lax.all_gather(dproj, 'tensor', axis=0, tiled=True)]
    gather x0 -> x1, local copies, waits for them, and re-layouts: none -> 4.96 us  [ring_gather(): parts = jnp.stack(parts)[(index - jnp.arange(size)) % size]]
    psum x1, blocking collectives: 16.2 us -> 20.6 us  [shards(): count = lax.psum(jnp.sum(valid), ('outer', 'dp'))]
  transfers between devices with their start and end apart: 4 -> 6, of which waited for: 2 -> 4; matrix products, arithmetic and copies ran while one was open for 2% -> 6% of each run, Pallas kernels for 0% -> 0%
where the time goes in v1:
time: 341 us
  blocking collectives  134 us (39%)
  waiting for transfers between devices  125 us (37%)
  matrix products  31.4 us (9%)
  between operations  17.3 us (5%)
  local copies, waits for them, and re-layouts  13 us (4%)
  other arithmetic  10 us (3%)
  starting transfers between devices  9.95 us (3%)
    psum x1, blocking collectives, shards(): zsum, loss_sum = lax.psum((zsum, loss_part), ('outer', 'dp'))  104 us
    ppermute x3, waiting for transfers between devices, ring_gather(): parts.append(lax.ppermute(parts[-1], axis, forward))  78 us
    all_to_all x1, waiting for transfers between devices, shards(): lax.all_to_all(part, 'tensor', split_axis=0, concat_axis=0, tiled=True)  46.6 us
    psum x1, blocking collectives, shards(): count = lax.psum(jnp.sum(valid), ('outer', 'dp'))  20.6 us
    dot_general x1, matrix products, shards(): lax.dot_general(out_weight, attn, (((1,), (1,)), ((), ())), preferred_ele...  16.7 us
    dot_general x1, matrix products, shards(): jnp.dot(exchanged, lax.all_gather(attn, ('outer', 'dp'), axis=0, tiled=Tr...  14.6 us
    psum x1, blocking collectives, shards(): lax.psum(jnp.stack([jnp.sum(z * z, axis=0), jnp.sum(z * both, axis=0)]),...  8.97 us
  transfers between devices with their start and end apart: 6, of which 4 were waited for; matrix products, arithmetic and copies ran while one was open for 6% of the time, Pallas kernels for 0%

profile of v1, /device:TPU:0, one launch (start us, length us, event | category | flops | bytes accessed | tf_op | source)
XLA Modules:
  0.0 340.7 jit_solution(6954757311194164346)
XLA Ops:
  7.2 16.7 %convolution_convert_fusion = bf16[8192,256]{1,0:T(8,128)(2,1)} fusion(bf16[8192,2048]{1,0:T(8,128)(2,1)} %param.10, bf16[256,2048]{1,0:T(8,128)(2,1)} %param.9), kind=kOutput, calls=%fused_computation.1 | convolution fusion | flops 8592031744 | bytes 38797312 | tf_op jit(solution)/shard_map/dot_general | solution.py:34
  23.9 0.0 copy-start.1
  23.9 0.0 copy-start.4
  23.9 0.0 copy-start.6
  23.9 0.0 copy-start.2
  23.9 0.0 copy-start.3
  23.9 5.3 %all-to-all-start = ((bf16[4,2048,256]{2,1,0:T(8,128)(2,1)}), bf16[4,2048,256]{2,1,0:T(8,128)(2,1)}, u32[]{:S(2)}, u32[]{:S(2)}) async-start(bf16[4,2048,256]{2,1,0:T(8,128)(2,1)} %bitcast.37), calls=%async_computation | async-start | bytes 8388608 | tf_op jit(solution)/shard_map/all_to_all | solution.py:36
  29.3 0.0 all-gather.2.cloned.1.call-start
  29.3 0.7 all-gather.2.cloned.1.call-update
  30.0 0.0 copy-done.1
  30.0 0.5 copy.16
  30.6 0.0 copy-done.4
  31.2 0.0 copy-done.6
  31.3 0.0 copy-done.2
  31.3 0.0 copy-done.3
  31.3 0.0 copy-start.5
  31.3 46.6 %all-to-all-done = bf16[4,2048,256]{2,1,0:T(8,128)(2,1)} async-done(((bf16[4,2048,256]{2,1,0:T(8,128)(2,1)}), bf16[4,2048,256]{2,1,0:T(8,128)(2,1)}, u32[]{:S(2)}, u32[]{:S(2)}) %all-to-all-start) | async-done | bytes 4194336 | tf_op jit(solution)/shard_map/all_to_all | solution.py:36
  77.9 3.0 convert_reduce_fusion
  80.9 0.4 multiply_reduce_fusion.2
  81.3 9.0 %psum.28 = f32[2,256]{1,0:T(2,128)S(1)} all-reduce(f32[2,256]{1,0:T(2,128)S(1)} %pad_maximum_fusion.1), channel_id=1, replica_groups=mesh['outer'=2,'dp'=4,'tensor'=4] {'tensor'}, use_global_device_ids=true, to_apply=%region_3.0 | all-reduce | flops 512 | bytes 4096 | tf_op jit(solution)/shard_map/psum | solution.py:41
  90.3 0.2 multiply_reduce_fusion.4
  90.5 0.2 multiply_reduce_fusion.6
  90.7 0.0 copy-done.5
  90.7 0.6 convert_reduce_fusion.1
  91.3 20.6 %psum.30 = f32[]{:T(128)} all-reduce(f32[]{:T(128)} %get-tuple-element.6), channel_id=1, replica_groups=mesh['outer'=2,'dp'=4,'tensor'=4] {'outer','dp'}, use_global_device_ids=true, to_apply=%region_9.10 | all-reduce | flops 1 | bytes 8 | tf_op jit(solution)/shard_map/psum | solution.py:33
  111.9 0.7 fusion.11
  112.5 0.1 multiply_reduce_fusion.5
  112.6 0.1 multiply_reduce_fusion.3
  112.7 0.8 subtract_convert_fusion
  113.5 0.0 copy-start
  113.5 1.1 copy-done
  114.6 0.0 collective-permute-start
  114.6 26.7 %collective-permute-done = bf16[2048,256]{1,0:T(8,128)(2,1)S(1)} collective-permute-done((bf16[2048,256]{1,0:T(8,128)(2,1)S(1)}, bf16[2048,256]{1,0:T(8,128)(2,1)S(1)}, u32[]{:S(2)}, u32[]{:S(2)}) %collective-permute-start) | collective-permute-done | bytes 1048608 | tf_op jit(solution)/shard_map/ppermute | solution.py:18
  141.3 0.0 collective-permute-start.1
  141.3 26.1 %collective-permute-done.1 = bf16[2048,256]{1,0:T(8,128)(2,1)S(1)} collective-permute-done((bf16[2048,256]{1,0:T(8,128)(2,1)S(1)}, bf16[2048,256]{1,0:T(8,128)(2,1)S(1)}, u32[]{:S(2)}, u32[]{:S(2)}) %collective-permute-start.1) | collective-permute-done | bytes 1048608 | tf_op jit(solution)/shard_map/ppermute | solution.py:18
  167.4 0.0 collective-permute-start.2
  167.4 25.2 %collective-permute-done.2 = bf16[2048,256]{1,0:T(8,128)(2,1)S(1)} collective-permute-done((bf16[2048,256]{1,0:T(8,128)(2,1)S(1)}, bf16[2048,256]{1,0:T(8,128)(2,1)S(1)}, u32[]{:S(2)}, u32[]{:S(2)}) %collective-permute-start.2) | collective-permute-done | bytes 1048608 | tf_op jit(solution)/shard_map/ppermute | solution.py:18
  192.6 3.3 pad_maximum_fusion
  195.9 5.0 %gather_fusion = bf16[4,2048,256]{2,1,0:T(8,128)(2,1)} fusion(bf16[4,2048,256]{2,1,0:T(8,128)(2,1)} %pad_maximum_fusion, s32[1024]{0:T(1024)S(1)} %pad_clamp_fusion), kind=kCustom, calls=%fused_computation | custom fusion | bytes 8388624 | tf_op jit(solution)/shard_map/gather | solution.py:20
  200.9 4.6 %all-to-all-start.1 = ((bf16[8,1024,256]{2,1,0:T(8,128)(2,1)}), bf16[8,1024,256]{2,1,0:T(8,128)(2,1)}, u32[]{:S(2)}, u32[]{:S(2)}) async-start(bf16[8,1024,256]{2,1,0:T(8,128)(2,1)} %bitcast.36), calls=%async_computation.1 | async-start | bytes 8388608 | tf_op jit(solution)/shard_map/all_to_all | solution.py:64
  205.5 104.2 %all-reduce = (f32[]{:T(128)}, f32[2048]{0:T(1024)S(1)}) all-reduce(f32[]{:T(128)} %get-tuple-element.7, f32[2048]{0:T(1024)S(1)} %get-tuple-element.11), channel_id=1, replica_groups=mesh['outer'=2,'dp'=4,'tensor'=4] {'outer','dp'}, use_global_device_ids=true, to_apply=%region_7.8 | all-reduce | flops 2049 | bytes 16392 | tf_op jit(solution)/shard_map/psum | solution.py:70
  311.0 0.6 convert_multiply_fusion
  311.6 0.0 all-to-all-done.1
  311.6 6.5 %copy.17 = bf16[1024,8,256]{0,2,1:T(8,128)(2,1)} copy(bf16[1024,8,256]{2,0,1:T(8,128)(2,1)} %bitcast.18) | data formatting | bytes 8388608 | tf_op jit(solution)/shard_map/all_to_all | solution.py:64
  318.1 0.0 all-gather.2.cloned.1.call-done
  318.1 14.6 %fusion.13 = f32[1024,2048]{1,0:T(8,128)} fusion(bf16[1024,2048]{0,1:T(8,128)(2,1)} %bitcast.38, bf16[2048,2048]{1,0:T(8,128)(2,1)} %all-gather.2.cloned.1.call-done), kind=kOutput, calls=%fused_computation.53 | convolution fusion | flops 8589934592 | bytes 20971520 | tf_op jit(solution)/shard_map/dot_general | solution.py:65
  (9 shorter events, 0.1 us)
Async XLA Ops:
  23.9 6.1 %copy-start.1 = (bf16[256,2048]{1,0:T(8,128)(2,1)S(1)}, bf16[256,2048]{1,0:T(8,128)(2,1)}, u32[]{:S(2)}) copy-start(bf16[256,2048]{1,0:T(8,128)(2,1)} %param.11) | copy-start | bytes 3145732
  23.9 6.6 %copy-start.4 = (s32[4]{0:T(128)S(1)}, s32[4]{0:T(128)}, u32[]{:S(2)}) copy-start(s32[4]{0:T(128)} %param.14) | copy-start | bytes 52
  23.9 7.3 %copy-start.6 = (s32[4,2]{0,1:T(2,128)S(1)}, s32[4,2]{0,1:T(2,128)}, u32[]{:S(2)}) copy-start(s32[4,2]{0,1:T(2,128)} %param.15) | copy-start | bytes 100
  23.9 7.3 %copy-start.2 = (bf16[2048]{0:T(1024)(128)(2,1)S(1)}, bf16[2048]{0:T(1024)(128)(2,1)}, u32[]{:S(2)}) copy-start(bf16[2048]{0:T(1024)(128)(2,1)} %param.12) | copy-start | bytes 12292
  23.9 7.3 %copy-start.3 = (bf16[2048]{0:T(1024)(128)(2,1)S(1)}, bf16[2048]{0:T(1024)(128)(2,1)}, u32[]{:S(2)}) copy-start(bf16[2048]{0:T(1024)(128)(2,1)} %param.13) | copy-start | bytes 12292
  23.9 53.9 %all-to-all-start = ((bf16[4,2048,256]{2,1,0:T(8,128)(2,1)}), bf16[4,2048,256]{2,1,0:T(8,128)(2,1)}, u32[]{:S(2)}, u32[]{:S(2)}) async-start(bf16[4,2048,256]{2,1,0:T(8,128)(2,1)} %bitcast.37), calls=%async_computation | async-start | bytes 8388608 | tf_op jit(solution)/shard_map/all_to_all | solution.py:36
  29.3 288.8 %all-gather.2.cloned.1.call-start = ((), (), s32[]{:S(2)}) async-start(), calls=%async_computation.2 | async-start | bytes 9437184 | tf_op jit(solution)/shard_map/all_gather | solution.py:67
  31.3 59.4 %copy-start.5 = (s32[4]{0:T(128)S(1)}, s32[4]{0:T(128)}, u32[]{:S(2)}) copy-start(s32[4]{0:T(128)} %param.16) | copy-start | bytes 52
  113.5 1.1 copy-start
  114.6 26.7 %collective-permute-start = (bf16[2048,256]{1,0:T(8,128)(2,1)S(1)}, bf16[2048,256]{1,0:T(8,128)(2,1)S(1)}, u32[]{:S(2)}, u32[]{:S(2)}) collective-permute-start(bf16[2048,256]{1,0:T(8,128)(2,1)S(1)} %get-tuple-element.10), channel_id=1, source_target_pairs={{0,1},{1,2},{2,3},{3,0},{4,5},{5,6},{6,7},{7,4},{8,9},{9,10},{10,1... | collective-permute-start | bytes 3145736 | tf_op jit(solution)/shard_map/ppermute | solution.py:18
  141.3 26.1 %collective-permute-start.1 = (bf16[2048,256]{1,0:T(8,128)(2,1)S(1)}, bf16[2048,256]{1,0:T(8,128)(2,1)S(1)}, u32[]{:S(2)}, u32[]{:S(2)}) collective-permute-start(bf16[2048,256]{1,0:T(8,128)(2,1)S(1)} %collective-permute-done), channel_id=1, source_target_pairs={{0,1},{1,2},{2,3},{3,0},{4,5},{5,6},{6,7},{7,4},{8,9},{9,10},{10,1... | collective-permute-start | bytes 3145736 | tf_op jit(solution)/shard_map/ppermute | solution.py:18
  167.4 25.2 %collective-permute-start.2 = (bf16[2048,256]{1,0:T(8,128)(2,1)S(1)}, bf16[2048,256]{1,0:T(8,128)(2,1)S(1)}, u32[]{:S(2)}, u32[]{:S(2)}) collective-permute-start(bf16[2048,256]{1,0:T(8,128)(2,1)S(1)} %collective-permute-done.1), channel_id=1, source_target_pairs={{0,1},{1,2},{2,3},{3,0},{4,5},{5,6},{6,7},{7,4},{8,9},{9,10},{10,1... | collective-permute-start | bytes 3145736 | tf_op jit(solution)/shard_map/ppermute | solution.py:18
  200.9 110.7 %all-to-all-start.1 = ((bf16[8,1024,256]{2,1,0:T(8,128)(2,1)}), bf16[8,1024,256]{2,1,0:T(8,128)(2,1)}, u32[]{:S(2)}, u32[]{:S(2)}) async-start(bf16[8,1024,256]{2,1,0:T(8,128)(2,1)} %bitcast.36), calls=%async_computation.1 | async-start | bytes 8388608 | tf_op jit(solution)/shard_map/all_to_all | solution.py:64
Sparse Core Ops, SparseCore 0:
  31.7 85.4 all-gather.1
